TPU v7x, 32 devices: a whole 2x2x4 slice. The times are simulated.
32 devices in a mesh: level: 4 (over z), dev: 8 (over y, x, core).
Axes of the slice: x: 2, y: 2, z: 4, core: 2. Of those that a mesh axis runs over, the one named last changes fastest.
Arguments:
- fields: float32 [4, 128, 12, 128], P('level', 'dev'), may hold values from -6 to 6
- own_src: int32 [4, 128], P('level', 'dev'), may hold values from 0 to 15
- own_weight: bfloat16 [4, 128, 128, 128], P('level', 'dev'), may hold values from 0 to 1, as said below
- send_block: int32 [4, 8, 8, 2], P('level', 'dev'), may hold values from 0 to 15
- send_target: int32 [4, 8, 8, 2], P('level', 'dev'), may hold values from 0 to 15
- send_count: int32 [4, 8, 8], P('level', 'dev'), may hold values from 0 to 2, as said below
- send_weight: bfloat16 [4, 8, 8, 2, 128, 128], P('level', 'dev'), may hold values from 0 to 1, as said below
- left_block: int32 [4, 8, 4, 2], P('level', 'dev'), may hold values from 0 to 15
- left_target: int32 [4, 8, 4, 2], P('level', 'dev'), may hold values from 0 to 15
- left_count: int32 [4, 8, 4], P('level', 'dev'), may hold values from 0 to 2, as said below
- left_weight: bfloat16 [4, 8, 4, 2, 128, 128], P('level', 'dev'), may hold values from 0 to 1, as said below
Outputs:
- remapped: float32 [4, 128, 12, 128], P('level', 'dev')
- totals: float32 [12], replicated
Inputs may be any that keep to these rules, and one draw needn't show every extreme that they name: send_count[l, s, s] = 0; for every level some receiver device gets 2 live slots from every other device of the level. left_count[m, q, m] = 0; for every device index some receiver level gets 2 live slots from every other level. `own_weight`: nonnegative; entry [k, i] is zero where old cell k and new cell i differ by more than 3; each column sums to a positive intersect fraction of at most 1. `send_weight`: nonnegative; entry [k, i] is zero where old cell k and new cell i differ by more than 3; each column sums to a positive intersect fraction of at most 1. `left_weight`: nonnegative; entry [k, i] is zero where old cell k and new cell i differ by more than 3; each column sums to a positive intersect fraction of at most 1.
All inputs are finite; a program needn't handle non-finite values.
Results may differ from a plain program's by a relative error of at most 0.0045.
Values may be sent and summed in bfloat16 or wider, within the bound.
No kernel may reach another device: no remote copies, remote signals or barrier semaphores. Data moves between devices by JAX's collectives and lax.ppermute only.
A program may use at most 64 MiB of HBM per device.

v0:
```python
import jax
import jax.numpy as jnp
from jax import lax
from jax.sharding import PartitionSpec as P


def pick_donors(rounded, block_index, count):
    donors = rounded[block_index]
    slots = block_index.shape[1]
    valid = lax.broadcasted_iota(jnp.int32, (1, slots), 1) < count[:, None]
    return jnp.where(valid[:, :, None, None], donors, jnp.zeros_like(donors))


def apply_weights(donors, weights):
    return jnp.einsum("pcmk,pcki->pcmi", donors, weights, preferred_element_type=jnp.float32)


def place_terms(contrib, target, blocks):
    comp = contrib.shape[2]
    cells = contrib.shape[3]
    flat_target = target.reshape(-1)
    onehot = (flat_target[:, None] == lax.broadcasted_iota(jnp.int32, (1, blocks), 1)).astype(
        jnp.float32
    )
    return jnp.einsum(
        "sb,smi->bmi", onehot, contrib.reshape(-1, comp, cells), precision=lax.Precision.HIGHEST
    )


def body(
    fields,
    own_src,
    own_weight,
    send_block,
    send_target,
    send_count,
    send_weight,
    left_block,
    left_target,
    left_count,
    left_weight,
):
    local = fields[0]
    blocks = local.shape[0]
    rounded = local.astype(jnp.bfloat16)
    own = jnp.einsum(
        "bmk,bki->bmi", rounded[own_src[0]], own_weight[0], preferred_element_type=jnp.float32
    )
    donors = pick_donors(rounded, send_block[0, 0], send_count[0, 0])
    strays = pick_donors(rounded, left_block[0, 0], left_count[0, 0])
    intra_terms, intra_target = (
        lax.all_to_all(
            apply_weights(donors, send_weight[0, 0]), "dev", split_axis=0, concat_axis=0, tiled=True
        ),
        lax.all_to_all(send_target[0, 0], "dev", split_axis=0, concat_axis=0, tiled=True),
    )
    left_terms, left_where = (
        lax.all_to_all(
            apply_weights(strays, left_weight[0, 0]),
            "level",
            split_axis=0,
            concat_axis=0,
            tiled=True,
        ),
        lax.all_to_all(left_target[0, 0], "level", split_axis=0, concat_axis=0, tiled=True),
    )
    remapped = (
        own
        + place_terms(intra_terms, intra_target, blocks)
        + place_terms(left_terms, left_where, blocks)
    )
    sums = lax.psum(jnp.sum(remapped, axis=(0, 2)), ("level", "dev"))
    totals = sums / (remapped.shape[2] * blocks)
    return (remapped[None], totals)


def solution(mesh):
    in_specs = (
        P("level", "dev", None, None),
        P("level", "dev"),
        P("level", "dev", None, None),
        P("level", "dev", None, None),
        P("level", "dev", None, None),
        P("level", "dev", None),
        P("level", "dev", None, None, None, None),
        P("level", "dev", None, None),
        P("level", "dev", None, None),
        P("level", "dev", None),
        P("level", "dev", None, None, None, None),
    )
    out_specs = (P("level", "dev", None, None), P())
    return jax.shard_map(body, mesh=mesh, in_specs=in_specs, out_specs=out_specs, check_vma=False)
```

profile of v0, /device:TPU:0, one launch (start us, length us, event | category | flops | bytes accessed | tf_op | source)
XLA Modules:
  0.0 84.1 jit_solution(18198775144529475194)
XLA Ops:
  0.7 0.7 copy-done.3
  1.4 0.6 copy.41
  2.0 6.3 %all-to-all-start.2 = ((s32[4,1,2]{2,1,0:T(1,128)}), s32[4,1,2]{2,1,0:T(1,128)S(1)}, u32[]{:S(2)}, u32[]{:S(2)}) async-start(s32[4,1,2]{2,1,0:T(1,128)} %copy.41), calls=%async_computation.2 | async-start | bytes 4096 | tf_op jit(solution)/shard_map/all_to_all | solution.py:65
  8.4 0.7 fusion.21
  9.0 0.7 iota_compare_fusion.3
  9.8 0.7 compare_select_fusion.1
  10.4 0.7 iota_compare_fusion.2
  11.2 0.7 compare_select_fusion
  12.2 1.3 %copy.36 = s32[8,1,2]{2,1,0:T(1,128)} copy(s32[8,1,2]{0,2,1:T(2,128)} %bitcast.53) | data formatting | bytes 128 | tf_op jit(solution)/shard_map/all_to_all | solution.py:55
  13.6 0.9 %copy.52 = bf16[1,16,12,128]{3,2,1,0:T(8,128)(2,1)S(1)} copy(f32[1,16,12,128]{3,1,2,0:T(8,128)} %param.11) | data formatting | bytes 147456 | tf_op args[0]
  15.1 0.6 gather_fusion.1
  16.2 3.7 %all-to-all-start = ((s32[8,1,2]{2,1,0:T(1,128)}), s32[8,1,2]{2,1,0:T(1,128)S(1)}, u32[]{:S(2)}, u32[]{:S(2)}) async-start(s32[8,1,2]{2,1,0:T(1,128)} %copy.36), calls=%async_computation | async-start | bytes 8192 | tf_op jit(solution)/shard_map/all_to_all | solution.py:55
  19.9 0.6 copy.43
  20.6 4.0 %all-to-all-done = s32[8,1,2]{2,1,0:T(1,128)S(1)} async-done(((s32[8,1,2]{2,1,0:T(1,128)}), s32[8,1,2]{2,1,0:T(1,128)S(1)}, u32[]{:S(2)}, u32[]{:S(2)}) %all-to-all-start) | async-done | bytes 96 | tf_op jit(solution)/shard_map/all_to_all | solution.py:55
  24.5 5.1 %all-to-all-start.3 = ((f32[4,2,12,128]{3,1,2,0:T(2,128)}), f32[4,2,12,128]{3,1,2,0:T(2,128)S(1)}, u32[]{:S(2)}, u32[]{:S(2)}) async-start(f32[4,2,12,128]{3,1,2,0:T(2,128)} %copy.43), calls=%async_computation.3 | async-start | bytes 98304 | tf_op jit(solution)/shard_map/all_to_all | solution.py:58
  29.6 0.6 gather_fusion
  30.2 0.7 copy.38
  31.4 0.7 reduce.6
  32.2 0.7 reduce.7
  32.9 2.4 %all-to-all-done.3 = f32[4,2,12,128]{3,1,2,0:T(2,128)S(1)} async-done(((f32[4,2,12,128]{3,1,2,0:T(2,128)}), f32[4,2,12,128]{3,1,2,0:T(2,128)S(1)}, u32[]{:S(2)}, u32[]{:S(2)}) %all-to-all-start.3) | async-done | bytes 49184 | tf_op jit(solution)/shard_map/all_to_all | solution.py:58
  35.3 3.4 %all-to-all-start.1 = ((f32[8,2,12,128]{3,1,2,0:T(2,128)}), f32[8,2,12,128]{3,1,2,0:T(2,128)S(1)}, u32[]{:S(2)}, u32[]{:S(2)}) async-start(f32[8,2,12,128]{3,1,2,0:T(2,128)} %copy.38), calls=%async_computation.1 | async-start | bytes 196608 | tf_op jit(solution)/shard_map/all_to_all | solution.py:52
  39.0 4.8 %all-to-all-done.1 = f32[8,2,12,128]{3,1,2,0:T(2,128)S(1)} async-done(((f32[8,2,12,128]{3,1,2,0:T(2,128)}), f32[8,2,12,128]{3,1,2,0:T(2,128)S(1)}, u32[]{:S(2)}, u32[]{:S(2)}) %all-to-all-start.1) | async-done | bytes 98336 | tf_op jit(solution)/shard_map/all_to_all | solution.py:52
  44.4 38.5 %psum.7 = f32[12]{0:T(128)S(1)} all-reduce(f32[12]{0:T(128)S(1)} %get-tuple-element.8), channel_id=1, replica_groups=mesh['level'=4,'dev'=8] {'level','dev'}, use_global_device_ids=true, to_apply=%region_1.2 | all-reduce | flops 12 | bytes 96 | tf_op jit(solution)/shard_map/psum | solution.py:72
  83.4 0.7 copy.46
  (27 shorter events, 3.6 us)
Async XLA Ops:
  0.6 43.4 %copy-start = (bf16[1,16,128,128]{3,2,1,0:T(8,128)(2,1)S(1)}, bf16[1,16,128,128]{3,2,1,0:T(8,128)(2,1)}, u32[]{:S(2)}) copy-start(bf16[1,16,128,128]{3,2,1,0:T(8,128)(2,1)} %param.13) | copy-start | bytes 1572868
  0.6 0.7 copy-start.3
  0.7 15.0 %copy-start.2 = (bf16[1,1,4,2,128,128]{5,4,3,2,1,0:T(8,128)(2,1)S(1)}, bf16[1,1,4,2,128,128]{5,4,3,2,1,0:T(8,128)(2,1)}, u32[]{:S(2)}) copy-start(bf16[1,1,4,2,128,128]{5,4,3,2,1,0:T(8,128)(2,1)} %param.21) | copy-start | bytes 786436
  0.7 15.2 %copy-start.1 = (bf16[1,1,8,2,128,128]{5,4,3,2,1,0:T(8,128)(2,1)S(1)}, bf16[1,1,8,2,128,128]{5,4,3,2,1,0:T(8,128)(2,1)}, u32[]{:S(2)}) copy-start(bf16[1,1,8,2,128,128]{5,4,3,2,1,0:T(8,128)(2,1)} %param.17) | copy-start | bytes 1572868
  2.0 14.2 %all-to-all-start.2 = ((s32[4,1,2]{2,1,0:T(1,128)}), s32[4,1,2]{2,1,0:T(1,128)S(1)}, u32[]{:S(2)}, u32[]{:S(2)}) async-start(s32[4,1,2]{2,1,0:T(1,128)} %copy.41), calls=%async_computation.2 | async-start | bytes 4096 | tf_op jit(solution)/shard_map/all_to_all | solution.py:65
  16.2 8.3 %all-to-all-start = ((s32[8,1,2]{2,1,0:T(1,128)}), s32[8,1,2]{2,1,0:T(1,128)S(1)}, u32[]{:S(2)}, u32[]{:S(2)}) async-start(s32[8,1,2]{2,1,0:T(1,128)} %copy.36), calls=%async_computation | async-start | bytes 8192 | tf_op jit(solution)/shard_map/all_to_all | solution.py:55
  24.5 10.8 %all-to-all-start.3 = ((f32[4,2,12,128]{3,1,2,0:T(2,128)}), f32[4,2,12,128]{3,1,2,0:T(2,128)S(1)}, u32[]{:S(2)}, u32[]{:S(2)}) async-start(f32[4,2,12,128]{3,1,2,0:T(2,128)} %copy.43), calls=%async_computation.3 | async-start | bytes 98304 | tf_op jit(solution)/shard_map/all_to_all | solution.py:58
  35.3 8.5 %all-to-all-start.1 = ((f32[8,2,12,128]{3,1,2,0:T(2,128)}), f32[8,2,12,128]{3,1,2,0:T(2,128)S(1)}, u32[]{:S(2)}, u32[]{:S(2)}) async-start(f32[8,2,12,128]{3,1,2,0:T(2,128)} %copy.38), calls=%async_computation.1 | async-start | bytes 196608 | tf_op jit(solution)/shard_map/all_to_all | solution.py:52
where the time goes:
time: 84.7 us; the launch traced here: 84.1 us
  blocking collectives  38.5 us (45%)
  starting transfers between devices  18.5 us (22%)
  waiting for transfers between devices  11.2 us (13%)
  local copies, waits for them, and re-layouts  8.43 us (10%)
  other arithmetic  5.33 us (6%)
  matrix products  1.38 us (2%)
    psum x1, blocking collectives, body(): sums = lax.psum(jnp.sum(remapped, axis=(0, 2)), ('level', 'dev'))  38.5 us
    all_to_all x1, starting transfers between devices, body(): lax.all_to_all(left_target[0, 0], 'level', split_axis=0, concat_axis=0, t...  6.35 us
    all_to_all x1, starting transfers between devices, body(): lax.all_to_all(apply_weights(strays, left_weight[0, 0]), 'level', split_a...  5.09 us
    all_to_all x1, waiting for transfers between devices, body(): lax.all_to_all(apply_weights(donors, send_weight[0, 0]), 'dev', split_axi...  4.79 us
    all_to_all x1, waiting for transfers between devices, body(): lax.all_to_all(send_target[0, 0], 'dev', split_axis=0, concat_axis=0, til...  3.97 us
    all_to_all x1, starting transfers between devices, body(): lax.all_to_all(send_target[0, 0], 'dev', split_axis=0, concat_axis=0, til...  3.74 us
    all_to_all x1, starting transfers between devices, body(): lax.all_to_all(apply_weights(donors, send_weight[0, 0]), 'dev', split_axi...  3.36 us
    all_to_all x1, waiting for transfers between devices, body(): lax.all_to_all(apply_weights(strays, left_weight[0, 0]), 'level', split_a...  2.42 us
  transfers between devices with their start and end apart: 4, of which 3 were waited for; matrix products, arithmetic and copies ran while one was open for 14% of the time, Pallas kernels for 0%

commit v1 on v0

v1 whole, which is shorter than its diff:
```python
import functools

import jax
import jax.numpy as jnp
from jax import lax
from jax.experimental import pallas as pl
from jax.experimental.pallas import tpu as pltpu
from jax.sharding import PartitionSpec as P

LANES = 128
TILE = 16


def up(value, step):
    return -(-value // step) * step


class Plan:
    def __init__(self, levels, peers, blocks, comp, cells, cap, lcap):
        self.levels, self.peers, self.blocks = levels, peers, blocks
        self.comp, self.cells, self.cap, self.lcap = comp, cells, cap, lcap
        self.slots = max(cap, lcap)
        self.width = self.slots * TILE
        self.per_group = LANES // self.width
        self.dev_groups = -(-peers // self.per_group)
        self.lev_groups = -(-levels // self.per_group)
        self.groups = self.dev_groups + self.lev_groups
        spare = TILE - comp
        self.sum_row = comp
        if self.groups <= spare:
            self.target_row = (self.slots - 1) * TILE + comp
            self.rows = self.width
        else:
            self.target_row = self.width
            self.rows = self.width + up(self.groups, TILE)
        assert comp + 3 <= TILE and self.slots >= 2 and cells == LANES


def first_kernel(
    plan,
    fields_hbm,
    own_src_hbm,
    own_weight_hbm,
    send_block_hbm,
    send_target_hbm,
    send_count_hbm,
    send_weight_hbm,
    left_block_hbm,
    left_target_hbm,
    left_count_hbm,
    left_weight_hbm,
    own_ref,
    msg_ref,
    fields_v,
    donors,
    own_weight,
    send_weight,
    left_weight,
    own_src,
    send_block,
    send_target,
    send_count,
    left_block,
    left_target,
    left_count,
    sems,
):
    blocks, comp = plan.blocks, plan.comp
    pairs = (
        (fields_hbm, fields_v),
        (own_src_hbm, own_src),
        (send_block_hbm, send_block),
        (send_target_hbm, send_target),
        (send_count_hbm, send_count),
        (left_block_hbm, left_block),
        (left_target_hbm, left_target),
        (left_count_hbm, left_count),
        (send_weight_hbm, send_weight),
        (left_weight_hbm, left_weight),
        (own_weight_hbm, own_weight),
    )
    copies = [pltpu.make_async_copy(src, dst, sems.at[i]) for i, (src, dst) in enumerate(pairs)]
    for copy in copies:
        copy.start()

    level = lax.axis_index("level")
    dev = lax.axis_index("dev")
    row = lax.broadcasted_iota(jnp.int32, (TILE, LANES), 0)
    lane = lax.broadcasted_iota(jnp.int32, (TILE, LANES), 1)
    part = lane % plan.width // TILE
    group_lane = lane // plan.width

    copies[0].wait()
    donors[...] = jnp.zeros_like(donors)
    for b in range(blocks):
        donors[b, 0:comp, :] = fields_v[pl.ds(b, comp, stride=blocks), :].astype(jnp.bfloat16)
    for copy in copies[1:8]:
        copy.wait()

    def term(block, weight):
        return jnp.dot(donors[block], weight, preferred_element_type=jnp.float32)

    sums = jnp.zeros((TILE, LANES), jnp.float32)
    dev_terms = []
    copies[8].wait()
    for p in range(plan.peers):
        terms = []
        for c in range(plan.cap):
            block = jnp.where(c < send_count[0, p], send_block[c, p], blocks)
            terms.append(term(block, send_weight[p * plan.cap + c]))
            sums += terms[-1]
        dev_terms.append(terms)
    lev_terms = []
    copies[9].wait()
    for p in range(plan.levels):
        terms = []
        for c in range(plan.lcap):
            block = jnp.where(c < left_count[0, p], left_block[c, p], blocks)
            terms.append(term(block, left_weight[p * plan.lcap + c]))
            sums += terms[-1]
        lev_terms.append(terms)
    copies[10].wait()
    for b in range(blocks):
        mine = term(own_src[0, b], own_weight[b])
        sums += mine
        own_ref[pl.ds(b, comp, stride=blocks), :] = mine[0:comp]

    total = jnp.sum(sums, axis=1, keepdims=True)
    total = jnp.sum(jnp.where(row == lane, total, 0.0), axis=0, keepdims=True)
    high = total.astype(jnp.bfloat16).astype(jnp.float32)
    rest = total - high
    middle = rest.astype(jnp.bfloat16).astype(jnp.float32)
    low = rest - middle
    sum_rows = jnp.where(
        row == plan.sum_row,
        high,
        jnp.where(row == plan.sum_row + 1, middle, jnp.where(row == plan.sum_row + 2, low, 0.0)),
    )

    def target_tile(group, offset, targets, base):
        value = jnp.zeros((TILE, LANES), jnp.int32)
        for c, target in enumerate(targets):
            value = jnp.where(part == c, target, value)
        here = (row + base == plan.target_row + group) & (group_lane == offset)
        return jnp.where(here, value, 0).astype(jnp.float32)

    def write(index, terms, targets, group, offset):
        for c in range(plan.slots):
            data = terms[c] if c < len(terms) else jnp.zeros((TILE, LANES), jnp.float32)
            if c == 0:
                data = data + sum_rows
            if plan.target_row // TILE == c:
                data = data + target_tile(group, offset, targets, c * TILE)
            msg_ref[index, c * TILE : (c + 1) * TILE, :] = data.astype(jnp.bfloat16)
        for r in range(plan.width, plan.rows, TILE):
            msg_ref[index, r : r + TILE, :] = target_tile(group, offset, targets, r).astype(
                jnp.bfloat16
            )

    meta = sum_rows.astype(jnp.bfloat16)
    for index in range(plan.levels * plan.peers):
        msg_ref[index, 0:TILE, :] = meta
    for p in range(plan.peers):
        write(
            level * plan.peers + p,
            dev_terms[p],
            [send_target[c, p] for c in range(plan.cap)],
            dev // plan.per_group,
            dev % plan.per_group,
        )
    for p in range(plan.levels):
        write(
            p * plan.peers + dev,
            lev_terms[p],
            [left_target[c, p] for c in range(plan.lcap)],
            plan.dev_groups + level // plan.per_group,
            level % plan.per_group,
        )


def second_kernel(plan, own_ref, msg_ref, out_ref, totals_ref, picked):
    blocks, comp = plan.blocks, plan.comp
    level = lax.axis_index("level")
    dev = lax.axis_index("dev")

    def gather(first, count, index_of):
        targets = jnp.zeros((plan.rows - plan.target_row // TILE * TILE, LANES), jnp.float32)
        span = up(count, plan.per_group)
        for s in range(span):
            at = (first * plan.per_group + s) * plan.width
            if s < count:
                picked[at : at + plan.width, :] = msg_ref[index_of(s), 0 : plan.width, :]
                targets += msg_ref[
                    index_of(s), plan.target_row // TILE * TILE : plan.rows, :
                ].astype(jnp.float32)
            else:
                picked[at : at + plan.width, :] = jnp.zeros((plan.width, LANES), jnp.bfloat16)
        return targets

    dev_targets = gather(0, plan.peers, lambda s: level * plan.peers + s)
    lev_targets = gather(plan.dev_groups, plan.levels, lambda s: s * plan.peers + dev)

    block_row = lax.broadcasted_iota(jnp.int32, (blocks, LANES), 0).astype(jnp.float32)
    lane = lax.broadcasted_iota(jnp.int32, (blocks, LANES), 1)
    one = jnp.ones((blocks, LANES), jnp.float32)
    zero = jnp.zeros((blocks, LANES), jnp.float32)
    placed = jnp.zeros((comp * blocks, LANES), jnp.float32)
    for g in range(plan.groups):
        targets = dev_targets if g < plan.dev_groups else lev_targets
        r = plan.target_row % TILE + g
        match = jnp.where(block_row == targets[r : r + 1, :], one, zero)
        select = jnp.concatenate(
            [jnp.where(lane % TILE == m, match, zero) for m in range(comp)], axis=0
        ).astype(jnp.bfloat16)
        placed += jnp.dot(
            select, picked[g * LANES : (g + 1) * LANES, :], preferred_element_type=jnp.float32
        )
    out_ref[...] = own_ref[...] + placed

    sums = jnp.zeros((TILE, LANES), jnp.float32)
    for index in range(plan.levels * plan.peers):
        sums += msg_ref[index, 0:TILE, :].astype(jnp.float32)
    r = plan.sum_row
    total = sums[r : r + 1, :] + sums[r + 1 : r + 2, :] + sums[r + 2 : r + 3, :]
    totals_ref[...] = (total * (1.0 / (plan.cells * blocks)))[0, :comp]


def body(
    fields,
    own_src,
    own_weight,
    send_block,
    send_target,
    send_count,
    send_weight,
    left_block,
    left_target,
    left_count,
    left_weight,
):
    blocks, comp, cells = fields.shape[1:]
    peers, cap = send_block.shape[2:]
    levels, lcap = left_block.shape[2:]
    plan = Plan(levels, peers, blocks, comp, cells, cap, lcap)
    rows = comp * blocks
    in_hbm = pl.BlockSpec(memory_space=pltpu.HBM)
    vmem = pl.BlockSpec(memory_space=pltpu.VMEM)
    own, message = pl.pallas_call(
        functools.partial(first_kernel, plan),
        out_shape=(
            jax.ShapeDtypeStruct((rows, cells), jnp.float32),
            jax.ShapeDtypeStruct((levels * peers, plan.rows, cells), jnp.bfloat16),
        ),
        in_specs=[in_hbm] * 11,
        out_specs=(vmem, vmem),
        scratch_shapes=[
            pltpu.VMEM((rows, cells), jnp.float32),
            pltpu.VMEM((blocks + 1, TILE, cells), jnp.bfloat16),
            pltpu.VMEM((blocks, cells, cells), jnp.bfloat16),
            pltpu.VMEM((peers * cap, cells, cells), jnp.bfloat16),
            pltpu.VMEM((levels * lcap, cells, cells), jnp.bfloat16),
            pltpu.SMEM((1, blocks), jnp.int32),
            pltpu.SMEM((cap, peers), jnp.int32),
            pltpu.SMEM((cap, peers), jnp.int32),
            pltpu.SMEM((1, peers), jnp.int32),
            pltpu.SMEM((lcap, levels), jnp.int32),
            pltpu.SMEM((lcap, levels), jnp.int32),
            pltpu.SMEM((1, levels), jnp.int32),
            pltpu.SemaphoreType.DMA((11,)),
        ],
        compiler_params=pltpu.CompilerParams(vmem_limit_bytes=24 * 2**20),
        name="terms",
    )(*(pltpu.with_memory_space_constraint(x, pltpu.HBM) for x in (
        fields[0].transpose(1, 0, 2).reshape(rows, cells),
        own_src,
        own_weight[0],
        send_block[0, 0].T,
        send_target[0, 0].T,
        send_count[0],
        send_weight[0, 0].reshape(peers * cap, cells, cells),
        left_block[0, 0].T,
        left_target[0, 0].T,
        left_count[0],
        left_weight[0, 0].reshape(levels * lcap, cells, cells),
    )))
    message = lax.all_to_all(message, ("level", "dev"), split_axis=0, concat_axis=0, tiled=True)
    remapped, totals = pl.pallas_call(
        functools.partial(second_kernel, plan),
        out_shape=(
            jax.ShapeDtypeStruct((rows, cells), jnp.float32),
            jax.ShapeDtypeStruct((comp,), jnp.float32),
        ),
        in_specs=[vmem, vmem],
        out_specs=(vmem, vmem),
        scratch_shapes=[pltpu.VMEM((plan.groups * LANES, cells), jnp.bfloat16)],
        compiler_params=pltpu.CompilerParams(vmem_limit_bytes=24 * 2**20),
        name="place",
    )(own, message)
    remapped = remapped.reshape(comp, blocks, cells).transpose(1, 0, 2)
    return (remapped[None], totals)


def solution(mesh):
    in_specs = (
        P("level", "dev", None, None),
        P("level", "dev"),
        P("level", "dev", None, None),
        P("level", "dev", None, None),
        P("level", "dev", None, None),
        P("level", "dev", None),
        P("level", "dev", None, None, None, None),
        P("level", "dev", None, None),
        P("level", "dev", None, None),
        P("level", "dev", None),
        P("level", "dev", None, None, None, None),
    )
    out_specs = (P("level", "dev", None, None), P())
    return jax.shard_map(body, mesh=mesh, in_specs=in_specs, out_specs=out_specs, check_vma=False)
```

time: 84.7 us -> 21.4 us (0.25)
  blocking collectives: 38.5 us -> 17.7 us
  starting transfers between devices: 18.5 us -> 0 us
  waiting for transfers between devices: 11.2 us -> 0 us
  local copies, waits for them, and re-layouts: 8.43 us -> 0 us
  other arithmetic: 5.33 us -> 0 us
  Pallas kernels: 0 us -> 2.84 us
  matrix products: 1.38 us -> 0 us
    psum x1 -> x0, blocking collectives: 38.5 us -> none  [body(): sums = lax.psum(jnp.sum(remapped, axis=(0, 2)), ('level', 'dev'))]
    all_to_all x4 -> x0, starting transfers between devices: 18.5 us -> none  [the longest x1 6.35 us: body(): lax.all_to_all(left_target[0, 0], 'level', split_axis=0, concat_axis=0, t...]
    all_to_all x0 -> x1, blocking collectives: none -> 17.7 us  [body(): lax.all_to_all(message, ('level', 'dev'), split_axis=0, concat_axis=0, ti...]
    all_to_all x4 -> x0, waiting for transfers between devices: 11.2 us -> none  [the longest x1 4.79 us: body(): lax.all_to_all(apply_weights(donors, send_weight[0, 0]), 'dev', split_axi...]
    pallas_call x0 -> x2, Pallas kernels: none -> 2.84 us  [the longest x1 1.99 us: body(): pl.pallas_call(functools.partial(first_kernel, plan), out_shape=(jax.Shap...]
    all_to_all x5 -> x0, local copies, waits for them, and re-layouts: 2.56 us -> none  [the longest x1 1.35 us: body(): lax.all_to_all(send_target[0, 0], 'dev', split_axis=0, concat_axis=0, til...]
    unnamed x10 -> x0, local copies, waits for them, and re-layouts: 2.33 us -> none
    select_n x3 -> x0, other arithmetic: 2.02 us -> none  [the longest x2 1.36 us: pick_donors(): donors = rounded[block_index]]
  transfers between devices with their start and end apart: 4 -> 0, of which waited for: 3 -> 0; matrix products, arithmetic and copies ran while one was open for 14% -> 0% of each run, Pallas kernels for 0% -> 0%
where the time goes in v1:
time: 21.4 us; the launch traced here: 21.2 us
  blocking collectives  17.7 us (83%)
  Pallas kernels  2.84 us (13%)
  between operations  0.64 us (3%)
    all_to_all x1, blocking collectives, body(): lax.all_to_all(message, ('level', 'dev'), split_axis=0, concat_axis=0, ti...  17.7 us
    pallas_call x1, Pallas kernels, body(): pl.pallas_call(functools.partial(first_kernel, plan), out_shape=(jax.Shap...  1.99 us
    pallas_call x1, Pallas kernels, body(): pl.pallas_call(functools.partial(second_kernel, plan), out_shape=(jax.Sha...  0.84 us

profile of v1, /device:TPU:0, one launch (start us, length us, event | category | flops | bytes accessed | tf_op | source)
XLA Modules:
  0.0 21.2 jit_solution(7662221323449703908)
XLA Ops:
  0.6 2.0 %terms.1 = (f32[192,128]{1,0:T(8,128)S(1)}, bf16[32,32,128]{2,1,0:T(8,128)(2,1)S(1)}) custom-call(f32[192,128]{1,0:T(8,128)} %bitcast.30, s32[1,16]{1,0:T(1,128)} %own_src_hbm.1, bf16[16,128,128]{2,1,0:T(8,128)(2,1)} %bitcast.27, s32[2,8]{1,0:T(2,128)} %bitcast.31, s32[2,8]{1,0:T(2,128)} %bitcast.32, s32[1,8]{1,0:T(1,128)} %bitcast.35, ...), custom_call_target="tpu_custom_call" | custom-call | tf_op jit(solution)/shard_map/terms/pallas_call | solution.py:248
  2.6 17.7 %all_to_all.5.msg_ref = bf16[32,32,128]{2,1,0:T(8,128)(2,1)S(1)} all-to-all(bf16[32,32,128]{2,1,0:T(8,128)(2,1)S(1)} %get-tuple-element.7), channel_id=1, replica_groups=mesh['level'=4,'dev'=8] {'level','dev'}, dimensions={0} | all-to-all | bytes 524288 | tf_op jit(solution)/shard_map/all_to_all | solution.py:286
  20.3 0.8 %place.1 = (f32[192,128]{1,0:T(8,128)}, f32[12]{0:T(128)}) custom-call(f32[192,128]{1,0:T(8,128)S(1)} %get-tuple-element.6.own_ref, bf16[32,32,128]{2,1,0:T(8,128)(2,1)S(1)} %all_to_all.5.msg_ref), custom_call_target="tpu_custom_call" | custom-call | tf_op jit(solution)/shard_map/place/pallas_call | solution.py:287

commit v2 on v1

v2 whole, which is shorter than its diff:
```python
import functools

import jax
import jax.numpy as jnp
from jax import lax
from jax.experimental import pallas as pl
from jax.experimental.pallas import tpu as pltpu
from jax.sharding import PartitionSpec as P

LANES = 128
TILE = 16


def divide(x, n, bound):
    if n & (n - 1) == 0:
        return x >> (n.bit_length() - 1)
    factor = -(-(1 << 20) // n)
    assert bound * (factor * n - (1 << 20)) < 1 << 20 and bound * factor < 1 << 31
    return (x * factor) >> 20


class Plan:
    def __init__(self, levels, peers, blocks, comp, cells, cap, lcap):
        self.levels, self.peers, self.blocks = levels, peers, blocks
        self.comp, self.cells, self.cap = comp, cells, cap
        self.data = cap * comp
        self.rows = self.data + 2
        self.ahead = peers * self.rows
        self.total = levels * self.ahead
        self.ids = (peers + levels) * cap
        self.groups = -(-self.total // LANES)
        assert cap == lcap and comp <= TILE and cells == LANES
        assert self.ahead % TILE == 0 and self.ids <= LANES
        assert self.rows % 2 == 0 and 2 * TILE + comp <= LANES

    def lane_of(self, level, dev, donor_level, peer, slot):
        other = jnp.where(peer == dev, (self.peers + donor_level) * self.cap + slot, -1)
        return jnp.where(donor_level == level, peer * self.cap + slot, other)

    def slot_of(self, row):
        slot = jnp.zeros_like(row)
        for c in range(1, self.cap):
            slot += jnp.where(row >= c * self.comp, 1, 0)
        return slot


def first_kernel(
    plan,
    fields_hbm,
    own_src_hbm,
    own_weight_hbm,
    send_block_hbm,
    send_target_hbm,
    send_count_hbm,
    send_weight_hbm,
    left_block_hbm,
    left_target_hbm,
    left_count_hbm,
    left_weight_hbm,
    own_ref,
    msg_ref,
    place_ref,
    fields_v,
    donors,
    own_weight,
    send_weight,
    left_weight,
    wide,
    own_src,
    send_block,
    send_target,
    send_count,
    left_block,
    left_target,
    left_count,
    sems,
):
    blocks, comp, cap = plan.blocks, plan.comp, plan.cap
    pairs = (
        (fields_hbm, fields_v),
        (own_src_hbm, own_src),
        (send_block_hbm, send_block),
        (send_target_hbm, send_target),
        (send_count_hbm, send_count),
        (left_block_hbm, left_block),
        (left_target_hbm, left_target),
        (left_count_hbm, left_count),
        (send_weight_hbm, send_weight),
        (left_weight_hbm, left_weight),
        (own_weight_hbm, own_weight),
    )
    copies = [pltpu.make_async_copy(src, dst, sems.at[i]) for i, (src, dst) in enumerate(pairs)]
    for copy in copies:
        copy.start()

    level = lax.axis_index("level")
    dev = lax.axis_index("dev")

    lane = lax.broadcasted_iota(jnp.int32, (1, LANES), 1)
    for g in range(plan.groups):
        at = lane + g * LANES
        index = divide(at, plan.rows, plan.total + LANES)
        row = at - index * plan.rows
        donor_level = divide(index, plan.peers, plan.levels * plan.peers + LANES)
        peer = index - donor_level * plan.peers
        slot = plan.slot_of(row)
        at_lane = plan.lane_of(level, dev, donor_level, peer, slot)
        part = jnp.where((at_lane >= 0) & (row < plan.data), row - slot * comp, -1)
        part = jnp.where(at < plan.total, part, -1)
        place_ref[g : g + 1, :] = jnp.maximum(at_lane, 0)
        place_ref[plan.groups + g : plan.groups + g + 1, :] = part

    wide[...] = jnp.zeros_like(wide)

    copies[0].wait()
    donors[...] = jnp.zeros_like(donors)
    for b in range(blocks):
        donors[b, 0:comp, :] = fields_v[pl.ds(b, comp, stride=blocks), :].astype(jnp.bfloat16)
    for copy in copies[1:8]:
        copy.wait()

    row = lax.broadcasted_iota(jnp.int32, (TILE, LANES), 0)
    column = lax.broadcasted_iota(jnp.int32, (TILE, LANES), 1)

    def term(block, weight):
        return jnp.dot(donors[block], weight, preferred_element_type=jnp.float32)

    sums = jnp.zeros((TILE, LANES), jnp.float32)
    for count, block, target, weight, peers, here, message_of, copy in (
        (
            send_count,
            send_block,
            send_target,
            send_weight,
            plan.peers,
            dev,
            lambda p: level * plan.peers + p,
            copies[8],
        ),
        (
            left_count,
            left_block,
            left_target,
            left_weight,
            plan.levels,
            plan.peers + level,
            lambda p: p * plan.peers + dev,
            copies[9],
        ),
    ):
        copy.wait()
        for p in range(peers):
            first = message_of(p) * plan.rows
            targets = jnp.zeros((1, LANES), jnp.float32)
            for c in range(cap):
                donor = jnp.where(c < count[0, p], block[c, p], blocks)
                value = term(donor, weight[p * cap + c])
                sums += value
                wide[pl.ds(first + c * comp, comp), :] = value[0:comp]
                targets = jnp.where(
                    lane == here * cap + c, target[c, p].astype(jnp.float32), targets
                )
            wide[pl.ds(first + plan.data, 1), :] = targets
    copies[10].wait()
    for b in range(blocks):
        mine = term(own_src[0, b], own_weight[b])
        sums += mine
        own_ref[pl.ds(b, comp, stride=blocks), :] = mine[0:comp]

    total = jnp.sum(sums, axis=1, keepdims=True)
    high = total.astype(jnp.bfloat16).astype(jnp.float32)
    rest = total - high
    middle = rest.astype(jnp.bfloat16).astype(jnp.float32)
    low = rest - middle
    spread = jnp.where(column == row, high, 0.0)
    spread = jnp.where(column == row + TILE, middle, spread)
    spread = jnp.where(column == row + 2 * TILE, low, spread)
    sum_row = jnp.sum(spread, axis=0, keepdims=True)
    for index in range(plan.levels * plan.peers):
        at = index * plan.rows + plan.data + 1
        wide[at : at + 1, :] = sum_row
    msg_ref[...] = wide[...].astype(jnp.bfloat16)


def second_kernel(plan, own_ref, msg_ref, place_ref, out_ref, totals_ref):
    blocks, comp = plan.blocks, plan.comp
    spans = [
        (g, g * LANES, min(LANES, plan.total - g * LANES)) for g in range(plan.groups)
    ]

    found = {}
    for peer in range(plan.peers):
        at = peer * plan.rows + plan.data
        low = at // 8 * 8
        for donor_level in range(plan.levels):
            first = donor_level * plan.ahead + low
            part = msg_ref[first : first + 8, :].astype(jnp.float32)
            found[at - low] = found[at - low] + part if at - low in found else part
    meta = sum(part[at : at + 2, :] for at, part in found.items())

    targets = jnp.broadcast_to(meta[0:1, :], (blocks, LANES))
    block_row = lax.broadcasted_iota(jnp.int32, (blocks, LANES), 0).astype(jnp.float32)
    placed = own_ref[...]
    for g, at, size in spans:
        index = jnp.broadcast_to(place_ref[g : g + 1, :], (blocks, LANES))
        match = jnp.take_along_axis(targets, index, axis=1) == block_row
        at_part = plan.groups + g
        part = jnp.broadcast_to(place_ref[at_part : at_part + 1, :], (blocks, LANES))
        key = jnp.where(match, part, -1)
        select = jnp.concatenate(
            [jnp.where(key == m, 1.0, 0.0).astype(jnp.bfloat16) for m in range(comp)], axis=0
        )
        placed += jnp.dot(
            select[:, :size], msg_ref[at : at + size, :], preferred_element_type=jnp.float32
        )
    out_ref[...] = placed

    sums = meta[1:2, :]
    total = sums[:, 0:comp]
    total += sums[:, TILE : TILE + comp]
    total += sums[:, 2 * TILE : 2 * TILE + comp]
    totals_ref[...] = (total * (1.0 / (plan.cells * blocks)))[0]


def hbm(x):
    return pltpu.with_memory_space_constraint(x, pltpu.HBM)


def body(
    fields,
    own_src,
    own_weight,
    send_block,
    send_target,
    send_count,
    send_weight,
    left_block,
    left_target,
    left_count,
    left_weight,
):
    blocks, comp, cells = fields.shape[1:]
    peers, cap = send_block.shape[2:]
    levels, lcap = left_block.shape[2:]
    plan = Plan(levels, peers, blocks, comp, cells, cap, lcap)
    rows = comp * blocks
    devices = levels * peers
    in_hbm = pl.BlockSpec(memory_space=pltpu.HBM)
    vmem = pl.BlockSpec(memory_space=pltpu.VMEM)
    own, message, place = pl.pallas_call(
        functools.partial(first_kernel, plan),
        out_shape=(
            jax.ShapeDtypeStruct((rows, cells), jnp.float32),
            jax.ShapeDtypeStruct((plan.total, cells), jnp.bfloat16),
            jax.ShapeDtypeStruct((2 * plan.groups, LANES), jnp.int32),
        ),
        in_specs=[in_hbm] * 11,
        out_specs=(vmem, vmem, vmem),
        scratch_shapes=[
            pltpu.VMEM((rows, cells), jnp.float32),
            pltpu.VMEM((blocks + 1, TILE, cells), jnp.bfloat16),
            pltpu.VMEM((blocks, cells, cells), jnp.bfloat16),
            pltpu.VMEM((peers * cap, cells, cells), jnp.bfloat16),
            pltpu.VMEM((levels * lcap, cells, cells), jnp.bfloat16),
            pltpu.VMEM((plan.total, cells), jnp.float32),
            pltpu.SMEM((1, blocks), jnp.int32),
            pltpu.SMEM((cap, peers), jnp.int32),
            pltpu.SMEM((cap, peers), jnp.int32),
            pltpu.SMEM((1, peers), jnp.int32),
            pltpu.SMEM((lcap, levels), jnp.int32),
            pltpu.SMEM((lcap, levels), jnp.int32),
            pltpu.SMEM((1, levels), jnp.int32),
            pltpu.SemaphoreType.DMA((11,)),
        ],
        compiler_params=pltpu.CompilerParams(vmem_limit_bytes=24 * 2**20),
        name="terms",
    )(
        hbm(fields[0].transpose(1, 0, 2).reshape(rows, cells)),
        hbm(own_src),
        hbm(own_weight[0]),
        hbm(send_block[0, 0].T),
        hbm(send_target[0, 0].T),
        hbm(send_count[0]),
        hbm(send_weight[0, 0].reshape(peers * cap, cells, cells)),
        hbm(left_block[0, 0].T),
        hbm(left_target[0, 0].T),
        hbm(left_count[0]),
        hbm(left_weight[0, 0].reshape(levels * lcap, cells, cells)),
    )
    message = lax.all_to_all(
        message.reshape(devices * plan.rows // 2, 2, cells),
        ("level", "dev"),
        split_axis=0,
        concat_axis=0,
        tiled=True,
    ).reshape(plan.total, cells)
    remapped, totals = pl.pallas_call(
        functools.partial(second_kernel, plan),
        out_shape=(
            jax.ShapeDtypeStruct((rows, cells), jnp.float32),
            jax.ShapeDtypeStruct((comp,), jnp.float32),
        ),
        in_specs=[vmem, vmem, vmem],
        out_specs=(vmem, vmem),
        compiler_params=pltpu.CompilerParams(vmem_limit_bytes=24 * 2**20),
        name="place",
    )(own, message, place)
    remapped = remapped.reshape(comp, blocks, cells).transpose(1, 0, 2)
    return (remapped[None], totals)


def solution(mesh):
    in_specs = (
        P("level", "dev", None, None),
        P("level", "dev"),
        P("level", "dev", None, None),
        P("level", "dev", None, None),
        P("level", "dev", None, None),
        P("level", "dev", None),
        P("level", "dev", None, None, None, None),
        P("level", "dev", None, None),
        P("level", "dev", None, None),
        P("level", "dev", None),
        P("level", "dev", None, None, None, None),
    )
    out_specs = (P("level", "dev", None, None), P())
    return jax.shard_map(body, mesh=mesh, in_specs=in_specs, out_specs=out_specs, check_vma=False)
```

time: 21.4 us -> 20.3 us (0.949)
  blocking collectives: 17.7 us -> 16.6 us
    all_to_all x1, blocking collectives: 17.7 us -> 16.6 us  [body(): lax.all_to_all(message.reshape(devices * plan.rows // 2, 2, cells), ('lev...]
where the time goes in v2:
time: 20.3 us; the launch traced here: 20.2 us
  blocking collectives  16.6 us (82%)
  Pallas kernels  2.97 us (15%)
  between operations  0.64 us (3%)
    all_to_all x1, blocking collectives, body(): lax.all_to_all(message.reshape(devices * plan.rows // 2, 2, cells), ('lev...  16.6 us
    pallas_call x1, Pallas kernels, body(): pl.pallas_call(functools.partial(first_kernel, plan), out_shape=(jax.Shap...  2.01 us
    pallas_call x1, Pallas kernels, body(): pl.pallas_call(functools.partial(second_kernel, plan), out_shape=(jax.Sha...  0.96 us

profile of v2, /device:TPU:0, one launch (start us, length us, event | category | flops | bytes accessed | tf_op | source)
XLA Modules:
  0.0 20.2 jit_solution(5272375938143616741)
XLA Ops:
  0.6 2.0 %terms.1 = (f32[192,128]{1,0:T(8,128)S(1)}, bf16[832,128]{1,0:T(8,128)(2,1)S(1)}, s32[14,128]{1,0:T(8,128)S(1)}) custom-call(f32[192,128]{1,0:T(8,128)} %bitcast.34, s32[1,16]{1,0:T(1,128)} %own_src_hbm.1, bf16[16,128,128]{2,1,0:T(8,128)(2,1)} %bitcast.31, s32[2,8]{1,0:T(2,128)} %bitcast.35, s32[2,8]{1,0:T(2,128)} %bitcast.36, s32[1,8]{1,0:T(1,128)} %bitcast.39, ...), custom_call_target="tpu_custom_call" | custom-call | tf_op jit(solution)/shard_map/terms/pallas_call | solution.py:250
  2.7 16.6 %all_to_all.5 = bf16[416,2,128]{2,1,0:T(2,128)(2,1)S(1)} all-to-all(bf16[416,2,128]{2,1,0:T(2,128)(2,1)S(1)} %bitcast.30), channel_id=1, replica_groups=mesh['level'=4,'dev'=8] {'level','dev'}, dimensions={0} | all-to-all | bytes 425984 | tf_op jit(solution)/shard_map/all_to_all | solution.py:290
  19.2 1.0 %place.1 = (f32[192,128]{1,0:T(8,128)}, f32[12]{0:T(128)}) custom-call(f32[192,128]{1,0:T(8,128)S(1)} %get-tuple-element.7.own_ref, bf16[832,128]{1,0:T(8,128)(2,1)S(1)} %bitcast.29, s32[14,128]{1,0:T(8,128)S(1)} %get-tuple-element.9.place_ref), custom_call_target="tpu_custom_call" | custom-call | tf_op jit(solution)/shard_map/place/pallas_call | solution.py:297

commit v3 on v2

--- a/solution.py
+++ b/solution.py
@@ -9,6 +9,10 @@
 
 LANES = 128
 TILE = 16
+
+
+def up(value, step):
+    return -(-value // step) * step
 
 
 def divide(x, n, bound):
@@ -28,14 +32,16 @@
         self.ahead = peers * self.rows
         self.total = levels * self.ahead
         self.ids = (peers + levels) * cap
-        self.groups = -(-self.total // LANES)
+        self.window = up(self.rows + TILE - 2, TILE)
+        self.picked = self.ahead + levels * self.window
+        self.groups = -(-self.picked // LANES)
         assert cap == lcap and comp <= TILE and cells == LANES
         assert self.ahead % TILE == 0 and self.ids <= LANES
         assert self.rows % 2 == 0 and 2 * TILE + comp <= LANES
 
-    def lane_of(self, level, dev, donor_level, peer, slot):
-        other = jnp.where(peer == dev, (self.peers + donor_level) * self.cap + slot, -1)
-        return jnp.where(donor_level == level, peer * self.cap + slot, other)
+    def window_of(self, dev):
+        first = (dev * self.rows) // TILE * TILE
+        return pl.multiple_of(jnp.minimum(first, self.ahead - self.window), TILE)
 
     def slot_of(self, row):
         slot = jnp.zeros_like(row)
@@ -97,33 +103,48 @@
     dev = lax.axis_index("dev")
 
     lane = lax.broadcasted_iota(jnp.int32, (1, LANES), 1)
+    skip = dev * plan.rows - plan.window_of(dev)
     for g in range(plan.groups):
         at = lane + g * LANES
-        index = divide(at, plan.rows, plan.total + LANES)
-        row = at - index * plan.rows
-        donor_level = divide(index, plan.peers, plan.levels * plan.peers + LANES)
-        peer = index - donor_level * plan.peers
+        peer = divide(at, plan.rows, plan.picked + LANES)
+        row = at - peer * plan.rows
+        beyond = jnp.maximum(at - plan.ahead, 0)
+        donor_level = divide(beyond, plan.window, plan.picked + LANES)
+        other_row = beyond - donor_level * plan.window - skip
+        row = jnp.where(at < plan.ahead, row, other_row)
+        donor = jnp.where(at < plan.ahead, peer, plan.peers + donor_level)
         slot = plan.slot_of(row)
-        at_lane = plan.lane_of(level, dev, donor_level, peer, slot)
-        part = jnp.where((at_lane >= 0) & (row < plan.data), row - slot * comp, -1)
-        part = jnp.where(at < plan.total, part, -1)
-        place_ref[g : g + 1, :] = jnp.maximum(at_lane, 0)
-        place_ref[plan.groups + g : plan.groups + g + 1, :] = part
-
+        live = (row >= 0) & (row < plan.data) & (at < plan.picked)
+        place_ref[g : g + 1, :] = jnp.where(live, donor * cap + slot, 0)
+        place_ref[plan.groups + g : plan.groups + g + 1, :] = jnp.where(
+            live, row - slot * comp, -1
+        )
     wide[...] = jnp.zeros_like(wide)
 
     copies[0].wait()
     donors[...] = jnp.zeros_like(donors)
     for b in range(blocks):
         donors[b, 0:comp, :] = fields_v[pl.ds(b, comp, stride=blocks), :].astype(jnp.bfloat16)
-    for copy in copies[1:8]:
+    for copy in copies[1:10]:
         copy.wait()
 
     row = lax.broadcasted_iota(jnp.int32, (TILE, LANES), 0)
     column = lax.broadcasted_iota(jnp.int32, (TILE, LANES), 1)
 
-    def term(block, weight):
-        return jnp.dot(donors[block], weight, preferred_element_type=jnp.float32)
+    empty = jnp.zeros((TILE, LANES), jnp.bfloat16)
+
+    def terms(which, weights):
+        count = len(which)
+        rows = [
+            jnp.concatenate([donors[b] if i == j else empty for j in range(count)], axis=1)
+            for i, b in enumerate(which)
+        ]
+        out = jnp.dot(
+            jnp.concatenate(rows, axis=0),
+            weights.reshape(count * LANES, LANES),
+            preferred_element_type=jnp.float32,
+        )
+        return [out[i * TILE : (i + 1) * TILE] for i in range(count)]
 
     sums = jnp.zeros((TILE, LANES), jnp.float32)
     for count, block, target, weight, peers, here, message_of, copy in (
@@ -148,13 +169,12 @@
             copies[9],
         ),
     ):
-        copy.wait()
         for p in range(peers):
             first = message_of(p) * plan.rows
             targets = jnp.zeros((1, LANES), jnp.float32)
-            for c in range(cap):
-                donor = jnp.where(c < count[0, p], block[c, p], blocks)
-                value = term(donor, weight[p * cap + c])
+            which = [jnp.where(c < count[0, p], block[c, p], blocks) for c in range(cap)]
+            values = terms(which, weight[p * cap : (p + 1) * cap])
+            for c, value in enumerate(values):
                 sums += value
                 wide[pl.ds(first + c * comp, comp), :] = value[0:comp]
                 targets = jnp.where(
@@ -162,10 +182,12 @@
                 )
             wide[pl.ds(first + plan.data, 1), :] = targets
     copies[10].wait()
-    for b in range(blocks):
-        mine = term(own_src[0, b], own_weight[b])
-        sums += mine
-        own_ref[pl.ds(b, comp, stride=blocks), :] = mine[0:comp]
+    for first in range(0, blocks, 2):
+        which = range(first, min(first + 2, blocks))
+        values = terms([own_src[0, b] for b in which], own_weight[first : which.stop])
+        for b, mine in zip(which, values):
+            sums += mine
+            own_ref[pl.ds(b, comp, stride=blocks), :] = mine[0:comp]
 
     total = jnp.sum(sums, axis=1, keepdims=True)
     high = total.astype(jnp.bfloat16).astype(jnp.float32)
@@ -182,10 +204,18 @@
     msg_ref[...] = wide[...].astype(jnp.bfloat16)
 
 
-def second_kernel(plan, own_ref, msg_ref, place_ref, out_ref, totals_ref):
+def second_kernel(plan, own_ref, msg_ref, place_ref, out_ref, totals_ref, picked):
     blocks, comp = plan.blocks, plan.comp
+    mine = pl.multiple_of(lax.axis_index("level") * plan.ahead, TILE)
+    picked[0 : plan.ahead, :] = msg_ref[pl.ds(mine, plan.ahead), :]
+    first = plan.window_of(lax.axis_index("dev"))
+    for donor_level in range(plan.levels):
+        at = plan.ahead + donor_level * plan.window
+        picked[at : at + plan.window, :] = msg_ref[
+            pl.ds(pl.multiple_of(donor_level * plan.ahead + first, TILE), plan.window), :
+        ]
     spans = [
-        (g, g * LANES, min(LANES, plan.total - g * LANES)) for g in range(plan.groups)
+        (g, g * LANES, min(LANES, plan.picked - g * LANES)) for g in range(plan.groups)
     ]
 
     found = {}
@@ -211,7 +241,7 @@
             [jnp.where(key == m, 1.0, 0.0).astype(jnp.bfloat16) for m in range(comp)], axis=0
         )
         placed += jnp.dot(
-            select[:, :size], msg_ref[at : at + size, :], preferred_element_type=jnp.float32
+            select[:, :size], picked[at : at + size, :], preferred_element_type=jnp.float32
         )
     out_ref[...] = placed
 
@@ -302,6 +332,7 @@
         ),
         in_specs=[vmem, vmem, vmem],
         out_specs=(vmem, vmem),
+        scratch_shapes=[pltpu.VMEM((plan.picked, cells), jnp.bfloat16)],
         compiler_params=pltpu.CompilerParams(vmem_limit_bytes=24 * 2**20),
         name="place",
     )(own, message, place)

time: 20.3 us -> 20.1 us (level)
  Pallas kernels: 2.97 us -> 2.74 us
where the time goes in v3:
time: 20.1 us; the launch traced here: 19.9 us
  blocking collectives  16.6 us (83%)
  Pallas kernels  2.74 us (14%)
  between operations  0.64 us (3%)
    all_to_all x1, blocking collectives, body(): lax.all_to_all(message.reshape(devices * plan.rows // 2, 2, cells), ('lev...  16.6 us
    pallas_call x1, Pallas kernels, body(): pl.pallas_call(functools.partial(first_kernel, plan), out_shape=(jax.Shap...  1.83 us
    pallas_call x1, Pallas kernels, body(): pl.pallas_call(functools.partial(second_kernel, plan), out_shape=(jax.Sha...  0.91 us

profile of v3, /device:TPU:0, one launch (start us, length us, event | category | flops | bytes accessed | tf_op | source)
XLA Modules:
  0.0 19.9 jit_solution(7524643747852323489)
XLA Ops:
  0.6 1.8 %terms.1 = (f32[192,128]{1,0:T(8,128)S(1)}, bf16[832,128]{1,0:T(8,128)(2,1)S(1)}, s32[8,128]{1,0:T(8,128)S(1)}) custom-call(f32[192,128]{1,0:T(8,128)} %bitcast.34, s32[1,16]{1,0:T(1,128)} %own_src_hbm.1, bf16[16,128,128]{2,1,0:T(8,128)(2,1)} %bitcast.31, s32[2,8]{1,0:T(2,128)} %bitcast.35, s32[2,8]{1,0:T(2,128)} %bitcast.36, s32[1,8]{1,0:T(1,128)} %bitcast.39, ...), custom_call_target="tpu_custom_call" | custom-call | tf_op jit(solution)/shard_map/terms/pallas_call | solution.py:280
  2.5 16.6 %all_to_all.5 = bf16[416,2,128]{2,1,0:T(2,128)(2,1)S(1)} all-to-all(bf16[416,2,128]{2,1,0:T(2,128)(2,1)S(1)} %bitcast.30), channel_id=1, replica_groups=mesh['level'=4,'dev'=8] {'level','dev'}, dimensions={0} | all-to-all | bytes 425984 | tf_op jit(solution)/shard_map/all_to_all | solution.py:320
  19.0 0.9 %place.1 = (f32[192,128]{1,0:T(8,128)}, f32[12]{0:T(128)}) custom-call(f32[192,128]{1,0:T(8,128)S(1)} %get-tuple-element.7.own_ref, bf16[832,128]{1,0:T(8,128)(2,1)S(1)} %bitcast.29, s32[8,128]{1,0:T(8,128)S(1)} %get-tuple-element.9.place_ref), custom_call_target="tpu_custom_call" | custom-call | tf_op jit(solution)/shard_map/place/pallas_call | solution.py:327
